TPU v7x, 32 devices: a whole 2x2x4 slice. The times are simulated.
32 devices in a mesh: rot: 8 (over z, y), cls: 4 (over x, core).
Axes of the slice: x: 2, y: 2, z: 4, core: 2. Of those that a mesh axis runs over, the one named last changes fastest.
Arguments:
- particles: bfloat16 [128, 16384], P('rot'), may hold values from -64 to 64
- references: bfloat16 [48, 96, 16384], P('cls', 'rot'), may hold values from -0.046875 to 0.046875
- micrograph: int32 [8, 16], P('rot'), may hold values from 0 to 3, never falling along the last dimension, each value on 1 to 8 neighbouring positions
- ctf: float32 [32, 64], P('rot'), may hold values from -1 to 1
- prior_class: int32 [128], P('rot'), may hold values from 0 to 47
Outputs:
- class_scores: float32 [128, 48], P('rot', 'cls')
- best_score: float32 [128], P('rot')
- prior_score: float32 [128], P('rot')
Inputs may be any that keep to these rules, and one draw needn't show every extreme that they name: The entries of one row are the micrograph numbers of that index of rot in order, never falling; each of the 4 micrographs has 1 to 8 particles.
All inputs are finite; a program needn't handle non-finite values.
Results may differ from a plain program's by a relative error of at most 0.00095.
Values may be sent and summed in bfloat16 or wider, within the bound.
No kernel may reach another device: no remote copies, remote signals or barrier semaphores. Data moves between devices by JAX's collectives and lax.ppermute only.
A program may use at most 128 MiB of HBM per device.

v0:
```python
import jax
import jax.numpy as jnp
from jax import lax
from jax.sharding import PartitionSpec as P

CYCLES = 64
POLAR = 128


def body(particles, references, micrograph, ctf, prior_class):
    part_count = particles.shape[0]
    micro_count = ctf.shape[0]
    class_count = references.shape[0]
    angle_count = references.shape[1]
    features = particles.shape[1]
    rotation_count = lax.axis_size("rot")
    particle_spectra = particles.astype(jnp.float32).reshape(part_count, CYCLES, 2 * POLAR)
    rotation_energy = jnp.mean(particle_spectra * particle_spectra, axis=2)
    indicator_matrix = (
        micrograph[0][:, None] == jnp.arange(micro_count, dtype=jnp.int32)[None, :]
    ).astype(jnp.float32)
    score_totals = jnp.dot(indicator_matrix.T, rotation_energy, precision=lax.Precision.HIGHEST)
    counts = jnp.sum(indicator_matrix, axis=0)
    mean_power = score_totals / counts[:, None]
    scaling_coefficient = ctf * lax.rsqrt(mean_power + 1e-06)
    particle_scores = jnp.dot(
        indicator_matrix, scaling_coefficient, precision=lax.Precision.HIGHEST
    )
    whitened = (
        (particle_spectra * particle_scores[:, :, None])
        .reshape(part_count, features)
        .astype(jnp.bfloat16)
    )
    ref_table = references.reshape(class_count * angle_count, features)
    portion = lax.all_gather(whitened, "rot", axis=0, tiled=True)
    scored = lax.dot_general(
        ref_table, portion, (((1,), (1,)), ((), ())), preferred_element_type=jnp.float32
    )
    best_local = jnp.max(scored.reshape(class_count, angle_count, portion.shape[0]), axis=1)
    blocks = best_local.reshape(class_count, rotation_count, part_count)
    received = lax.all_to_all(blocks, "rot", split_axis=1, concat_axis=1, tiled=True)
    owned = jnp.max(received, axis=1)
    class_scores = owned.T
    local_best = jnp.max(class_scores, axis=1)
    class_index = lax.axis_index("cls") * class_count + jnp.arange(class_count, dtype=jnp.int32)
    chosen = prior_class[:, None] == class_index[None, :]
    local_prior = jnp.max(jnp.where(chosen, class_scores, -1e30), axis=1)
    best_score, prior_score = lax.pmax((local_best, local_prior), "cls")
    return (class_scores, best_score, prior_score)


def solution(mesh):
    in_specs = (P("rot", None), P("cls", "rot", None), P("rot", None), P("rot", None), P("rot"))
    out_specs = (P("rot", "cls"), P("rot"), P("rot"))
    return jax.shard_map(body, mesh=mesh, in_specs=in_specs, out_specs=out_specs, check_vma=False)
```

profile of v0, /device:TPU:0, one launch (start us, length us, event | category | flops | bytes accessed | tf_op | source)
XLA Modules:
  0.0 118.3 jit_solution(16492835034037239104)
XLA Ops:
  7.2 0.0 copy-start.2
  7.2 0.0 copy-start
  7.2 0.0 copy-start.3
  7.2 0.0 all-gather.2.cloned.1.call-start
  7.2 0.8 convert_reduce_fusion
  8.1 1.1 convert_multiply_fusion.1
  9.2 0.3 copy.13
  9.5 0.2 reduce_sum.18
  9.7 0.0 copy-done.2
  9.7 0.0 copy-done.3
  9.7 0.1 fusion.2
  9.9 0.2 fusion.6
  10.1 0.2 mul.26
  10.3 0.6 copy.14
  10.9 0.0 copy-done
  10.9 1.0 fusion.3
  11.9 0.0 all-gather.2.cloned.1.call-update
  11.9 6.7 %reshape.27 = bf16[144,16384]{1,0:T(8,128)(2,1)} reshape(bf16[12,12,16384]{2,1,0:T(8,128)(2,1)} %param.6) | data formatting | bytes 9437184 | tf_op jit(solution)/shard_map/reshape | solution.py:34
  18.6 0.0 copy-start.1
  18.6 68.9 %all-gather.2.cloned.1.call-done = bf16[128,16384]{1,0:T(8,128)(2,1)} async-done(((bf16[16,16384]{1,0:T(8,128)(2,1)}), bf16[128,16384]{1,0:T(8,128)(2,1)}) %all-gather.2.cloned.1.call-update) | async-done | bytes 4194320 | tf_op jit(solution)/shard_map/all_gather | solution.py:35
  87.6 5.0 %convolution_bitcast_fusion = f32[144,128]{1,0:T(8,128)S(1)} fusion(bf16[128,16384]{1,0:T(8,128)(2,1)} %all-gather.2.cloned.1.call-done, bf16[144,16384]{1,0:T(8,128)(2,1)} %reshape.27), kind=kOutput, calls=%fused_computation.2 | convolution fusion | flops 603979776 | bytes 8986624 | tf_op jit(solution)/shard_map/dot_general | solution.py:36
  92.6 0.1 reshape.29
  92.7 0.7 reshape.30
  93.4 3.3 %all-to-all-start = ((f32[8,1,192]{2,1,0:T(1,128)}), f32[8,1,192]{2,1,0:T(1,128)S(1)}, u32[]{:S(2)}, u32[]{:S(2)}) async-start(f32[8,1,192]{2,1,0:T(1,128)} %reshape.30), calls=%async_computation | async-start | bytes 16384 | tf_op jit(solution)/shard_map/all_to_all | solution.py:41
  96.8 6.4 %all-to-all-done = f32[8,1,192]{2,1,0:T(1,128)S(1)} async-done(((f32[8,1,192]{2,1,0:T(1,128)}), f32[8,1,192]{2,1,0:T(1,128)S(1)}, u32[]{:S(2)}, u32[]{:S(2)}) %all-to-all-start) | async-done | bytes 6176 | tf_op jit(solution)/shard_map/all_to_all | solution.py:41
  103.2 0.5 broadcast.9
  103.7 0.7 reduce.2
  104.4 0.1 reshape.31
  104.5 0.7 copy.12
  105.2 0.0 copy-done.1
  105.2 0.1 select_reduce_fusion
  105.3 6.2 %all-reduce = (f32[16]{0:T(128)}, f32[16]{0:T(128)}) all-reduce(f32[16]{0:T(128)S(1)} %get-tuple-element.9, f32[16]{0:T(128)S(1)} %select_reduce_fusion), channel_id=1, replica_groups=mesh['rot'=8,'cls'=4] {'cls'}, use_global_device_ids=true, to_apply=%region_5.6 | all-reduce | flops 32 | bytes 256 | tf_op jit(solution)/shard_map/pmax | solution.py:48
  (5 shorter events, 0.1 us)
Async XLA Ops:
  7.2 2.6 %copy-start.2 = (s32[1,16]{1,0:T(1,128)S(1)}, s32[1,16]{1,0:T(1,128)}, u32[]{:S(2)}) copy-start(s32[1,16]{1,0:T(1,128)} %param.7) | copy-start | bytes 196
  7.2 3.7 %copy-start = (bf16[16,16384]{1,0:T(8,128)(2,1)S(1)}, bf16[16,16384]{1,0:T(8,128)(2,1)}, u32[]{:S(2)}) copy-start(bf16[16,16384]{1,0:T(8,128)(2,1)} %param.5) | copy-start | bytes 1572868
  7.2 2.5 %copy-start.3 = (f32[4,64]{1,0:T(4,128)S(1)}, f32[4,64]{1,0:T(4,128)}, u32[]{:S(2)}) copy-start(f32[4,64]{1,0:T(4,128)} %param.8) | copy-start | bytes 3076
  7.2 80.4 %all-gather.2.cloned.1.call-start = ((), (), s32[]{:S(2)}) async-start(), calls=%async_computation.1 | async-start | bytes 4718592 | tf_op jit(solution)/shard_map/all_gather | solution.py:35
  18.6 86.6 %copy-start.1 = (s32[16]{0:T(128)S(1)}, s32[16]{0:T(128)}, u32[]{:S(2)}) copy-start(s32[16]{0:T(128)} %param.9) | copy-start | bytes 196
  93.4 9.8 %all-to-all-start = ((f32[8,1,192]{2,1,0:T(1,128)}), f32[8,1,192]{2,1,0:T(1,128)S(1)}, u32[]{:S(2)}, u32[]{:S(2)}) async-start(f32[8,1,192]{2,1,0:T(1,128)} %reshape.30), calls=%async_computation | async-start | bytes 16384 | tf_op jit(solution)/shard_map/all_to_all | solution.py:41
Sparse Core Ops, SparseCore 0:
  12.0 75.5 all-gather.1
where the time goes:
time: 119 us; the launch traced here: 118 us
  waiting for transfers between devices  75.4 us (63%)
  between operations  14.2 us (12%)
  local copies, waits for them, and re-layouts  9.95 us (8%)
  blocking collectives  6.17 us (5%)
  matrix products  5.32 us (4%)
  other arithmetic  3.92 us (3%)
  starting transfers between devices  3.37 us (3%)
    all_gather x1, waiting for transfers between devices, body(): portion = lax.all_gather(whitened, 'rot', axis=0, tiled=True)  68.9 us
    reshape x1, local copies, waits for them, and re-layouts, body(): ref_table = references.reshape(class_count * angle_count, features)  6.73 us
    all_to_all x1, waiting for transfers between devices, body(): lax.all_to_all(blocks, 'rot', split_axis=1, concat_axis=1, tiled=True)  6.45 us
    pmax x1, blocking collectives, body(): best_score, prior_score = lax.pmax((local_best, local_prior), 'cls')  6.17 us
    dot_general x1, matrix products, body(): lax.dot_general(ref_table, portion, (((1,), (1,)), ((), ())), preferred_e...  5 us
    all_to_all x1, starting transfers between devices, body(): lax.all_to_all(blocks, 'rot', split_axis=1, concat_axis=1, tiled=True)  3.33 us
    unnamed x13, local copies, waits for them, and re-layouts  2.4 us
  transfers between devices with their start and end apart: 2, of which 2 were waited for; matrix products, arithmetic and copies ran while one was open for 6% of the time, Pallas kernels for 0%

commit v1 on v0

v1 whole, which is shorter than its diff:
```python
import functools

import jax
import jax.numpy as jnp
from jax import lax
from jax.experimental import pallas as pl
from jax.experimental.pallas import tpu as pltpu
from jax.sharding import PartitionSpec as P


EPS = 1e-06
NEG = -3.0e38
ROW = 16
GROUP = 8
MIB = 1 << 20

IN_SPECS = (P("rot", None), P("cls", "rot", None), P("rot", None), P("rot", None), P("rot"))
OUT_SPECS = (P("rot", "cls"), P("rot"), P("rot"))


def whiten_kernel(mic_ref, ctf_ref, p_ref, w_ref, q_ref, h_ref):
    n, features = p_ref.shape
    micros, cycles = ctf_ref.shape
    per = features // cycles
    lane = lax.broadcasted_iota(jnp.int32, (n, cycles), 1)
    power = jnp.zeros((n, cycles), jnp.float32)
    for r in range(cycles):
        x = p_ref[:, r * per : (r + 1) * per].astype(jnp.float32)
        power = jnp.where(lane == r, jnp.sum(x * x, axis=1, keepdims=True), power)
    power = power * (1.0 / per)
    row = lax.broadcasted_iota(jnp.int32, (n, n), 0)
    col = lax.broadcasted_iota(jnp.int32, (n, n), 1)
    mic = jnp.broadcast_to(mic_ref[...].astype(jnp.float32), (n, n))
    owner = jnp.sum(jnp.where(row == col, mic, 0.0), axis=1, keepdims=True)
    factor = jnp.zeros((n, cycles), jnp.float32)
    for m in range(micros):
        member = owner == float(m)
        count = jnp.sum(jnp.where(member, 1.0, 0.0), axis=0, keepdims=True)
        total = jnp.sum(jnp.where(member, power, 0.0), axis=0, keepdims=True)
        scale = ctf_ref[m : m + 1, :] * lax.rsqrt(total / count + EPS)
        factor = jnp.where(member, scale, factor)
    for r in range(cycles):
        part = slice(r * per, (r + 1) * per)
        x = p_ref[:, part].astype(jnp.float32)
        w_ref[:, part] = (x * factor[:, r : r + 1]).astype(jnp.bfloat16)
    cls = lax.axis_index("cls")
    quarter = q_ref.shape[1]
    q_ref[...] = w_ref[:, pl.ds(pl.multiple_of(cls * quarter, quarter), quarter)]
    half = h_ref.shape[1]
    h_ref[...] = w_ref[:, pl.ds(pl.multiple_of((cls % 2) * half, half), half)]


def score_kernel(steps, *refs):
    w_ref, y_ref, cy_ref, *rest = refs
    pieces, (r_ref, o_ref, all_ref) = rest[:-3], rest[-3:]
    n, features = w_ref.shape
    classes, angles, _ = r_ref.shape
    half, quarter = features // 2, features // 4
    rot, cls = lax.axis_index("rot"), lax.axis_index("cls")
    z, y, x, c = rot // 2, rot % 2, cls // 2, cls % 2

    def put(piece, zz, yy, at, size):
        rows = pl.ds(pl.multiple_of((zz * 2 + yy) * n, n), n)
        all_ref[rows, pl.ds(pl.multiple_of(at * size, size), size)] = piece[...]

    put(w_ref, z, y, 0, features)
    put(y_ref, z, 1 - y, c, half)
    put(cy_ref, z, 1 - y, 1 - c, half)
    for i, k in enumerate(steps):
        zk = jnp.bitwise_xor(z, k)
        for j, (yy, xx) in enumerate(((y, x), (y, 1 - x), (1 - y, x), (1 - y, 1 - x))):
            own, other = pieces[8 * i + 2 * j], pieces[8 * i + 2 * j + 1]
            put(own, zk, yy, 2 * xx + c, quarter)
            put(other, zk, yy, 2 * xx + 1 - c, quarter)

    total = all_ref.shape[0]
    score = jnp.zeros((classes * ROW, total), jnp.float32)
    block = quarter // 2
    for b in range(features // block):
        part = slice(b * block, (b + 1) * block)
        rows = r_ref[:, :, part]
        rows = jnp.concatenate(
            [rows, jnp.zeros((classes, ROW - angles, block), rows.dtype)], axis=1
        ).reshape(classes * ROW, block)
        score += lax.dot_general(
            rows, all_ref[:, part], (((1,), (1,)), ((), ())), preferred_element_type=jnp.float32
        )
    best = jnp.max(score.reshape(classes, ROW, total)[:, :angles], axis=1)
    best = jnp.concatenate([best, jnp.zeros((ROW - classes, total), jnp.float32)], axis=0)
    sub = lax.broadcasted_iota(jnp.int32, (GROUP, total), 0)
    lanes = lax.broadcasted_iota(jnp.int32, (GROUP, total), 1) // n
    copies = o_ref.shape[0] // (total // n)
    for g in range(ROW // GROUP):
        a = best[g * GROUP : (g + 1) * GROUP]
        chunk = jnp.zeros_like(a)
        for d in range(GROUP):
            moved = pltpu.roll(pltpu.roll(a, (GROUP - d) % GROUP, 0), d * n, 1)
            chunk = jnp.where(lanes == (sub + d) % GROUP, moved, chunk)
        for holder in range(total // n):
            for copy in range(copies):
                o_ref[holder * copies + copy, :, g * total : (g + 1) * total] = chunk[
                    holder : holder + 1
                ]


def final_kernel(holders, classes, in_ref, prior_ref, scores_ref, best_ref, chosen_ref):
    blocks = in_ref.shape[0] // holders
    width = in_ref.shape[2]
    n = prior_ref.shape[1]
    got = []
    for b in range(blocks):
        row = in_ref[b]
        for h in range(1, holders):
            row = jnp.maximum(row, in_ref[h * blocks + b])
        got.append(row)
    lane = lax.broadcasted_iota(jnp.int32, (1, width), 1)
    cls_of = lane // n
    real = cls_of < classes
    cls = lax.axis_index("cls")
    prior = jnp.concatenate([prior_ref[...]] * (width // n), axis=1)
    own = jnp.zeros((1, width), jnp.float32)
    top = jnp.full((1, width), NEG, jnp.float32)
    chosen = jnp.full((1, width), NEG, jnp.float32)
    for b in range(blocks):
        own = jnp.where(cls == b, got[b], own)
        top = jnp.maximum(top, jnp.where(real, got[b], NEG))
        hit = jnp.logical_and(real, prior == cls_of + b * classes)
        chosen = jnp.maximum(chosen, jnp.where(hit, got[b], NEG))

    def fold(v):
        size = width
        while size > n:
            size //= 2
            v = jnp.maximum(v[:, :size], v[:, size : 2 * size])
        return v

    best_ref[...] = fold(top)
    chosen_ref[...] = fold(chosen)
    at = lax.broadcasted_iota(jnp.int32, (n, width), 0)
    lanes = lax.broadcasted_iota(jnp.int32, (n, width), 1)
    spread = jnp.where(lanes % n == at, jnp.broadcast_to(own, (n, width)), 0.0)
    column = lax.broadcasted_iota(jnp.int32, (n, classes), 1)
    scores = jnp.zeros((n, classes), jnp.float32)
    for k in range(classes):
        one = jnp.sum(jnp.where(lanes // n == k, spread, 0.0), axis=1, keepdims=True)
        scores = jnp.where(column == k, one, scores)
    scores_ref[...] = scores


def direct_body(rots, parts, particles, references, micrograph, ctf, prior_class):
    n, features = particles.shape
    classes = references.shape[0]
    vmem = pl.BlockSpec(memory_space=pltpu.VMEM)
    bf16 = functools.partial(jax.ShapeDtypeStruct, dtype=jnp.bfloat16)
    f32 = functools.partial(jax.ShapeDtypeStruct, dtype=jnp.float32)

    def to(change):
        pairs = []
        for r in range(rots):
            for s in range(parts):
                z, y, x, c = change(r // 2, r % 2, s // 2, s % 2)
                pairs.append((r * parts + s, (z * 2 + y) * parts + x * 2 + c))
        return pairs

    def send(value, change):
        return lax.ppermute(value, ("rot", "cls"), to(change))

    def over_x(z, y, x, c):
        return z, y, 1 - x, c

    def over_y(z, y, x, c):
        return z, 1 - y, x, c

    def over_both(z, y, x, c):
        return z, 1 - y, 1 - x, c

    def over_core(z, y, x, c):
        return z, y, x, 1 - c

    whitened, quarter, half = pl.pallas_call(
        whiten_kernel,
        out_shape=(bf16((n, features)), bf16((n, features // 4)), bf16((n, features // 2))),
        in_specs=[vmem] * 3,
        out_specs=(vmem,) * 3,
    )(micrograph, ctf, particles)
    steps = tuple(range(1, rots // 2))
    got = {}
    got["y"] = send(half, over_y)
    for k in steps:
        got[f"z{k}"] = send(quarter, lambda z, y, x, c, k=k: (z ^ k, y, x, c))
    for k in steps:
        first = got[f"z{k}"]
        got[f"x{k}"] = send(first, over_x)
        got[f"y{k}"] = send(first, over_y)
        if k < 3:
            got[f"f{k}"] = send(got[f"y{k}"], over_x)
        else:
            got[f"f{k}"] = send(first, over_both)
    for name in list(got):
        got["c" + name] = send(got[name], over_core)
    pieces = []
    for k in steps:
        for kind in "zxyf":
            pieces += [got[f"{kind}{k}"], got[f"c{kind}{k}"]]
    chunks = pl.pallas_call(
        functools.partial(score_kernel, steps),
        out_shape=f32((rots * parts, 1, ROW * n)),
        in_specs=[vmem] * (len(pieces) + 4),
        out_specs=vmem,
        scratch_shapes=[pltpu.VMEM((rots * n, features), jnp.bfloat16)],
        compiler_params=pltpu.CompilerParams(vmem_limit_bytes=32 * MIB),
    )(whitened, got["y"], got["cy"], *pieces, references)
    received = lax.all_to_all(chunks, ("rot", "cls"), 0, 0, tiled=True)
    scores, best, chosen = pl.pallas_call(
        functools.partial(final_kernel, rots, classes),
        out_shape=(f32((n, classes)), f32((1, n)), f32((1, n))),
        in_specs=[vmem] * 2,
        out_specs=(vmem,) * 3,
    )(received, prior_class.reshape(1, n))
    return scores, best.reshape(n), chosen.reshape(n)


def gathered_body(particles, references, micrograph, ctf, prior_class):
    n, features = particles.shape
    micros, cycles = ctf.shape
    classes, angles, _ = references.shape
    rots = lax.axis_size("rot")
    spectra = particles.astype(jnp.float32).reshape(n, cycles, features // cycles)
    power = jnp.mean(spectra * spectra, axis=2)
    member = micrograph[0][:, None] == jnp.arange(micros, dtype=jnp.int32)[None, :]
    member = member.astype(jnp.float32)
    total = jnp.dot(member.T, power, precision=lax.Precision.HIGHEST)
    mean_power = total / jnp.sum(member, axis=0)[:, None]
    scale = ctf * lax.rsqrt(mean_power + EPS)
    factor = jnp.dot(member, scale, precision=lax.Precision.HIGHEST)
    whitened = (spectra * factor[:, :, None]).reshape(n, features).astype(jnp.bfloat16)
    table = references.reshape(classes * angles, features)
    everyone = lax.all_gather(whitened, "rot", axis=0, tiled=True)
    scored = lax.dot_general(
        table, everyone, (((1,), (1,)), ((), ())), preferred_element_type=jnp.float32
    )
    local = jnp.max(scored.reshape(classes, angles, everyone.shape[0]), axis=1)
    blocks = local.reshape(classes, rots, n)
    received = lax.all_to_all(blocks, "rot", split_axis=1, concat_axis=1, tiled=True)
    class_scores = jnp.max(received, axis=1).T
    local_best = jnp.max(class_scores, axis=1)
    index = lax.axis_index("cls") * classes + jnp.arange(classes, dtype=jnp.int32)
    chosen = prior_class[:, None] == index[None, :]
    local_prior = jnp.max(jnp.where(chosen, class_scores, -1e30), axis=1)
    best_score, prior_score = lax.pmax((local_best, local_prior), "cls")
    return class_scores, best_score, prior_score


def solution(mesh):
    rots, parts = mesh.shape["rot"], mesh.shape["cls"]
    few = rots == GROUP and parts == 4
    body = functools.partial(direct_body, rots, parts) if few else gathered_body
    return jax.shard_map(
        body, mesh=mesh, in_specs=IN_SPECS, out_specs=OUT_SPECS, check_vma=False
    )
```

time: 119 us -> 65 us (0.55)
  waiting for transfers between devices: 75.4 us -> 20.6 us
  starting transfers between devices: 3.37 us -> 20.2 us
  between operations: 14.2 us -> 0.69 us
  blocking collectives: 6.17 us -> 13 us
  Pallas kernels: 0 us -> 6.36 us
  local copies, waits for them, and re-layouts: 9.95 us -> 3.83 us
  matrix products: 5.32 us -> 0 us
  other arithmetic: 3.92 us -> 0 us
    all_gather x1 -> x0, waiting for transfers between devices: 68.9 us -> none  [body(): portion = lax.all_gather(whitened, 'rot', axis=0, tiled=True)]
    ppermute x0 -> x26, waiting for transfers between devices: none -> 20.6 us  [send(): return lax.ppermute(value, ('rot', 'cls'), to(change))]
    ppermute x0 -> x26, starting transfers between devices: none -> 20.2 us  [send(): return lax.ppermute(value, ('rot', 'cls'), to(change))]
    all_to_all x0 -> x1, blocking collectives: none -> 13 us  [direct_body(): received = lax.all_to_all(chunks, ('rot', 'cls'), 0, 0, tiled=True)]
    reshape x4 -> x0, local copies, waits for them, and re-layouts: 6.82 us -> none  [the longest x1 6.73 us: body(): ref_table = references.reshape(class_count * angle_count, features)]
    all_to_all x1 -> x0, waiting for transfers between devices: 6.45 us -> none  [body(): lax.all_to_all(blocks, 'rot', split_axis=1, concat_axis=1, tiled=True)]
    pallas_call x0 -> x3, Pallas kernels: none -> 6.36 us  [the longest x1 2.57 us: direct_body(): pl.pallas_call(whiten_kernel, out_shape=(bf16((n, features)), bf16((n, fe...]
    pmax x1 -> x0, blocking collectives: 6.17 us -> none  [body(): best_score, prior_score = lax.pmax((local_best, local_prior), 'cls')]
  transfers between devices with their start and end apart: 2 -> 26, of which waited for: 2 -> 7; matrix products, arithmetic and copies ran while one was open for 6% -> 0% of each run, Pallas kernels for 0% -> 0%
where the time goes in v1:
time: 65 us; the launch traced here: 64.7 us
  waiting for transfers between devices  20.6 us (32%)
  starting transfers between devices  20.2 us (31%)
  blocking collectives  13 us (20%)
  Pallas kernels  6.36 us (10%)
  local copies, waits for them, and re-layouts  3.83 us (6%)
  between operations  0.69 us (1%)
    ppermute x26, waiting for transfers between devices, send(): return lax.ppermute(value, ('rot', 'cls'), to(change))  20.6 us
    ppermute x26, starting transfers between devices, send(): return lax.ppermute(value, ('rot', 'cls'), to(change))  20.2 us
    all_to_all x1, blocking collectives, direct_body(): received = lax.all_to_all(chunks, ('rot', 'cls'), 0, 0, tiled=True)  13 us
    unnamed x4, local copies, waits for them, and re-layouts  3.83 us
    pallas_call x1, Pallas kernels, direct_body(): pl.pallas_call(whiten_kernel, out_shape=(bf16((n, features)), bf16((n, fe...  2.57 us
    pallas_call x1, Pallas kernels, direct_body(): pl.pallas_call(functools.partial(score_kernel, steps), out_shape=f32((rot...  2.18 us
    pallas_call x1, Pallas kernels, direct_body(): pl.pallas_call(functools.partial(final_kernel, rots, classes), out_shape=...  1.61 us
  transfers between devices with their start and end apart: 26, of which 7 were waited for; matrix products, arithmetic and copies ran while one was open for 0% of the time, Pallas kernels for 0%

profile of v1, /device:TPU:0, one launch (start us, length us, event | category | flops | bytes accessed | tf_op | source)
XLA Modules:
  0.0 64.7 jit_solution(2043368435590629438)
XLA Ops:
  0.6 2.6 %shard_map.76 = (bf16[16,16384]{1,0:T(8,128)(2,1)}, bf16[16,4096]{1,0:T(8,128)(2,1)}, bf16[16,8192]{1,0:T(8,128)(2,1)}) custom-call(s32[1,16]{1,0:T(1,128)} %mic_ref.1, f32[4,64]{1,0:T(4,128)} %ctf_ref.1, bf16[16,16384]{1,0:T(8,128)(2,1)} %p_ref.1), custom_call_target="tpu_custom_call" | custom-call | tf_op jit(solution)/shard_map/pallas_call | solution.py:180
  3.2 5.1 %collective-permute-start.18 = (bf16[16,4096]{1,0:T(8,128)(2,1)}, bf16[16,4096]{1,0:T(8,128)(2,1)S(1)}, u32[]{:S(2)}, u32[]{:S(2)}) collective-permute-start(bf16[16,4096]{1,0:T(8,128)(2,1)} %get-tuple-element.11), channel_id=1, source_target_pairs={{0,24},{1,25},{2,26},{3,27},{4,28},{5,29},{6,30},{7,31},{8,16},{9,... | collective-permute-start | bytes 393224 | tf_op jit(solution)/shard_map/ppermute | solution.py:166
  8.3 0.0 collective-permute-start.10
  8.3 0.6 collective-permute-start.2
  8.8 4.1 %collective-permute-done.18.refs_19_ = bf16[16,4096]{1,0:T(8,128)(2,1)S(1)} collective-permute-done((bf16[16,4096]{1,0:T(8,128)(2,1)}, bf16[16,4096]{1,0:T(8,128)(2,1)S(1)}, u32[]{:S(2)}, u32[]{:S(2)}) %collective-permute-start.18) | collective-permute-done | bytes 131104 | tf_op jit(solution)/shard_map/ppermute | solution.py:166
  12.9 2.6 %collective-permute-start.24 = (bf16[16,4096]{1,0:T(8,128)(2,1)S(1)}, bf16[16,4096]{1,0:T(8,128)(2,1)S(1)}, u32[]{:S(2)}, u32[]{:S(2)}) collective-permute-start(bf16[16,4096]{1,0:T(8,128)(2,1)S(1)} %collective-permute-done.18.refs_19_), channel_id=1, source_target_pairs={{0,6},{1,7},{2,4},{3,5},{4,2},{5,3},{6,0},{7,1},{8,14},{9,15},{10,... | collective-permute-start | bytes 393224 | tf_op jit(solution)/shard_map/ppermute | solution.py:166
  15.6 0.5 collective-permute-start.22
  16.1 0.4 collective-permute-start.20
  16.4 3.1 %collective-permute-done.10.refs_11_ = bf16[16,4096]{1,0:T(8,128)(2,1)S(1)} collective-permute-done((bf16[16,4096]{1,0:T(8,128)(2,1)}, bf16[16,4096]{1,0:T(8,128)(2,1)S(1)}, u32[]{:S(2)}, u32[]{:S(2)}) %collective-permute-start.10) | collective-permute-done | bytes 131104 | tf_op jit(solution)/shard_map/ppermute | solution.py:166
  19.6 0.0 collective-permute-start.19
  19.6 0.0 collective-permute-done.2.refs_3_
  19.6 1.5 %collective-permute-start.14 = (bf16[16,4096]{1,0:T(8,128)(2,1)S(1)}, bf16[16,4096]{1,0:T(8,128)(2,1)S(1)}, u32[]{:S(2)}, u32[]{:S(2)}) collective-permute-start(bf16[16,4096]{1,0:T(8,128)(2,1)S(1)} %collective-permute-done.10.refs_11_), channel_id=1, source_target_pairs={{0,4},{1,5},{2,6},{3,7},{4,0},{5,1},{6,2},{7,3},{8,12},{9,13},{10,... | collective-permute-start | bytes 393224 | tf_op jit(solution)/shard_map/ppermute | solution.py:166
  21.1 0.0 collective-permute-done.24.refs_25_
  21.1 1.5 %collective-permute-start.12 = (bf16[16,4096]{1,0:T(8,128)(2,1)S(1)}, bf16[16,4096]{1,0:T(8,128)(2,1)S(1)}, u32[]{:S(2)}, u32[]{:S(2)}) collective-permute-start(bf16[16,4096]{1,0:T(8,128)(2,1)S(1)} %collective-permute-done.10.refs_11_), channel_id=1, source_target_pairs={{0,2},{1,3},{2,0},{3,1},{4,6},{5,7},{6,4},{7,5},{8,10},{9,11},{10,... | collective-permute-start | bytes 393224 | tf_op jit(solution)/shard_map/ppermute | solution.py:166
  22.6 0.0 collective-permute-done.22.refs_23_
  22.6 0.5 collective-permute-start
  23.1 0.0 collective-permute-done.20.refs_21_
  23.1 0.0 collective-permute-start.11
  23.1 0.0 collective-permute-done.19.refs_20_
  23.1 1.6 %collective-permute-start.6 = (bf16[16,4096]{1,0:T(8,128)(2,1)S(1)}, bf16[16,4096]{1,0:T(8,128)(2,1)S(1)}, u32[]{:S(2)}, u32[]{:S(2)}) collective-permute-start(bf16[16,4096]{1,0:T(8,128)(2,1)S(1)} %collective-permute-done.2.refs_3_), channel_id=1, source_target_pairs={{0,4},{1,5},{2,6},{3,7},{4,0},{5,1},{6,2},{7,3},{8,12},{9,13},{10,... | collective-permute-start | bytes 393224 | tf_op jit(solution)/shard_map/ppermute | solution.py:166
  24.7 0.9 %collective-permute-done.14.refs_15_ = bf16[16,4096]{1,0:T(8,128)(2,1)S(1)} collective-permute-done((bf16[16,4096]{1,0:T(8,128)(2,1)S(1)}, bf16[16,4096]{1,0:T(8,128)(2,1)S(1)}, u32[]{:S(2)}, u32[]{:S(2)}) %collective-permute-start.14) | collective-permute-done | bytes 131104 | tf_op jit(solution)/shard_map/ppermute | solution.py:166
  25.6 1.8 %collective-permute-start.4 = (bf16[16,4096]{1,0:T(8,128)(2,1)S(1)}, bf16[16,4096]{1,0:T(8,128)(2,1)S(1)}, u32[]{:S(2)}, u32[]{:S(2)}) collective-permute-start(bf16[16,4096]{1,0:T(8,128)(2,1)S(1)} %collective-permute-done.2.refs_3_), channel_id=1, source_target_pairs={{0,2},{1,3},{2,0},{3,1},{4,6},{5,7},{6,4},{7,5},{8,10},{9,11},{10,... | collective-permute-start | bytes 393224 | tf_op jit(solution)/shard_map/ppermute | solution.py:166
  27.5 0.0 collective-permute-done.12.refs_13_
  27.5 0.0 collective-permute-start.3
  27.5 0.0 collective-permute-done.11.refs_12_
  27.5 0.5 collective-permute-start.25
  28.0 5.9 %collective-permute-done.6.refs_7_ = bf16[16,4096]{1,0:T(8,128)(2,1)S(1)} collective-permute-done((bf16[16,4096]{1,0:T(8,128)(2,1)S(1)}, bf16[16,4096]{1,0:T(8,128)(2,1)S(1)}, u32[]{:S(2)}, u32[]{:S(2)}) %collective-permute-start.6) | collective-permute-done | bytes 131104 | tf_op jit(solution)/shard_map/ppermute | solution.py:166
  33.9 0.0 collective-permute-start.23
  33.9 0.0 collective-permute-done.4.refs_5_
  33.9 0.5 collective-permute-start.21
  34.4 0.0 collective-permute-done.3.refs_4_
  34.4 1.5 %collective-permute-start.16 = (bf16[16,4096]{1,0:T(8,128)(2,1)S(1)}, bf16[16,4096]{1,0:T(8,128)(2,1)S(1)}, u32[]{:S(2)}, u32[]{:S(2)}) collective-permute-start(bf16[16,4096]{1,0:T(8,128)(2,1)S(1)} %collective-permute-done.14.refs_15_), channel_id=1, source_target_pairs={{0,2},{1,3},{2,0},{3,1},{4,6},{5,7},{6,4},{7,5},{8,10},{9,11},{10,... | collective-permute-start | bytes 393224 | tf_op jit(solution)/shard_map/ppermute | solution.py:166
  35.9 0.0 collective-permute-done.refs_1_
  35.9 0.0 collective-permute-start.15
  35.9 0.0 collective-permute-done.25.refs_26_
  35.9 0.5 collective-permute-start.13
  36.5 0.0 collective-permute-done.23.refs_24_
  36.5 0.5 collective-permute-start.8
  37.0 0.0 collective-permute-done.21.refs_22_
  37.0 0.0 collective-permute-start.1
  37.0 3.7 %collective-permute-done.16.refs_17_ = bf16[16,4096]{1,0:T(8,128)(2,1)S(1)} collective-permute-done((bf16[16,4096]{1,0:T(8,128)(2,1)S(1)}, bf16[16,4096]{1,0:T(8,128)(2,1)S(1)}, u32[]{:S(2)}, u32[]{:S(2)}) %collective-permute-start.16) | collective-permute-done | bytes 131104 | tf_op jit(solution)/shard_map/ppermute | solution.py:166
  40.7 0.0 collective-permute-start.7
  40.7 0.0 collective-permute-done.15.refs_16_
  40.7 0.5 collective-permute-start.5
  41.2 0.0 collective-permute-done.13.refs_14_
  41.2 0.1 collective-permute-start.17
  41.3 1.4 %collective-permute-done.8.refs_9_ = bf16[16,4096]{1,0:T(8,128)(2,1)S(1)} collective-permute-done((bf16[16,4096]{1,0:T(8,128)(2,1)S(1)}, bf16[16,4096]{1,0:T(8,128)(2,1)S(1)}, u32[]{:S(2)}, u32[]{:S(2)}) %collective-permute-start.8) | collective-permute-done | bytes 131104 | tf_op jit(solution)/shard_map/ppermute | solution.py:166
  42.7 0.0 collective-permute-start.9
  42.7 0.0 collective-permute-done.7.refs_8_
  42.7 0.0 collective-permute-done.5.refs_6_
  42.7 0.0 collective-permute-done.17.refs_18_
  42.7 1.3 %collective-permute-done.9.refs_10_ = bf16[16,4096]{1,0:T(8,128)(2,1)S(1)} collective-permute-done((bf16[16,4096]{1,0:T(8,128)(2,1)S(1)}, bf16[16,4096]{1,0:T(8,128)(2,1)S(1)}, u32[]{:S(2)}, u32[]{:S(2)}) %collective-permute-start.9) | collective-permute-done | bytes 131104 | tf_op jit(solution)/shard_map/ppermute | solution.py:166
  44.1 0.0 collective-permute-done.1.refs_2_
  44.1 0.0 copy-start
  44.1 2.8 %copy-done = bf16[12,12,16384]{2,1,0:T(8,128)(2,1)S(1)} copy-done((bf16[12,12,16384]{2,1,0:T(8,128)(2,1)S(1)}, bf16[12,12,16384]{2,1,0:T(8,128)(2,1)}, u32[]{:S(2)}) %copy-start) | copy-done | bytes 4718616
  46.9 0.0 copy-start.1
  46.9 1.0 %copy-done.1 = bf16[16,16384]{1,0:T(8,128)(2,1)S(1)} copy-done((bf16[16,16384]{1,0:T(8,128)(2,1)S(1)}, bf16[16,16384]{1,0:T(8,128)(2,1)}, u32[]{:S(2)}) %copy-start.1) | copy-done | bytes 524312
  47.9 2.2 %shard_map.77 = f32[32,1,256]{2,1,0:T(1,128)S(1)} custom-call(bf16[16,16384]{1,0:T(8,128)(2,1)S(1)} %copy-done.1, bf16[16,8192]{1,0:T(8,128)(2,1)S(1)} %collective-permute-done.refs_1_, bf16[16,8192]{1,0:T(8,128)(2,1)S(1)} %collective-permute-done.1.refs_2_, bf16[16,4096]{1,0:T(8,128)(2,1)S(1)} %collective-permute-done.2.refs_3_, ...), custom_call_target="tpu_custom_call" | custom-call | tf_op jit(solution)/shard_map/pallas_call | solution.py:205
  50.1 13.0 %all_to_all.5.in_ref = f32[32,1,256]{2,1,0:T(1,128)} all-to-all(f32[32,1,256]{2,1,0:T(1,128)S(1)} %shard_map.77), channel_id=1, replica_groups=mesh['rot'=8,'cls'=4] {'rot','cls'}, dimensions={0} | all-to-all | bytes 65536 | tf_op jit(solution)/shard_map/all_to_all | solution.py:213
  63.1 1.6 %shard_map.78 = (f32[16,12]{1,0:T(8,128)}, f32[1,16]{1,0:T(1,128)}, f32[1,16]{1,0:T(1,128)}) custom-call(f32[32,1,256]{2,1,0:T(1,128)} %all_to_all.5.in_ref, s32[1,16]{1,0:T(1,128)} %bitcast.3), custom_call_target="tpu_custom_call" | custom-call | tf_op jit(solution)/shard_map/pallas_call | solution.py:214
Async XLA Ops:
  3.2 9.7 %collective-permute-start.18 = (bf16[16,4096]{1,0:T(8,128)(2,1)}, bf16[16,4096]{1,0:T(8,128)(2,1)S(1)}, u32[]{:S(2)}, u32[]{:S(2)}) collective-permute-start(bf16[16,4096]{1,0:T(8,128)(2,1)} %get-tuple-element.11), channel_id=1, source_target_pairs={{0,24},{1,25},{2,26},{3,27},{4,28},{5,29},{6,30},{7,31},{8,16},{9,... | collective-permute-start | bytes 393224 | tf_op jit(solution)/shard_map/ppermute | solution.py:166
  8.3 11.3 %collective-permute-start.10 = (bf16[16,4096]{1,0:T(8,128)(2,1)}, bf16[16,4096]{1,0:T(8,128)(2,1)S(1)}, u32[]{:S(2)}, u32[]{:S(2)}) collective-permute-start(bf16[16,4096]{1,0:T(8,128)(2,1)} %get-tuple-element.11), channel_id=1, source_target_pairs={{0,16},{1,17},{2,18},{3,19},{4,20},{5,21},{6,22},{7,23},{8,24},{9,... | collective-permute-start | bytes 393224 | tf_op jit(solution)/shard_map/ppermute | solution.py:166
  8.3 11.3 %collective-permute-start.2 = (bf16[16,4096]{1,0:T(8,128)(2,1)}, bf16[16,4096]{1,0:T(8,128)(2,1)S(1)}, u32[]{:S(2)}, u32[]{:S(2)}) collective-permute-start(bf16[16,4096]{1,0:T(8,128)(2,1)} %get-tuple-element.11), channel_id=1, source_target_pairs={{0,8},{1,9},{2,10},{3,11},{4,12},{5,13},{6,14},{7,15},{8,0},{9,1},... | collective-permute-start | bytes 393224 | tf_op jit(solution)/shard_map/ppermute | solution.py:166
  12.9 8.2 %collective-permute-start.24 = (bf16[16,4096]{1,0:T(8,128)(2,1)S(1)}, bf16[16,4096]{1,0:T(8,128)(2,1)S(1)}, u32[]{:S(2)}, u32[]{:S(2)}) collective-permute-start(bf16[16,4096]{1,0:T(8,128)(2,1)S(1)} %collective-permute-done.18.refs_19_), channel_id=1, source_target_pairs={{0,6},{1,7},{2,4},{3,5},{4,2},{5,3},{6,0},{7,1},{8,14},{9,15},{10,... | collective-permute-start | bytes 393224 | tf_op jit(solution)/shard_map/ppermute | solution.py:166
  15.6 7.1 %collective-permute-start.22 = (bf16[16,4096]{1,0:T(8,128)(2,1)S(1)}, bf16[16,4096]{1,0:T(8,128)(2,1)S(1)}, u32[]{:S(2)}, u32[]{:S(2)}) collective-permute-start(bf16[16,4096]{1,0:T(8,128)(2,1)S(1)} %collective-permute-done.18.refs_19_), channel_id=1, source_target_pairs={{0,4},{1,5},{2,6},{3,7},{4,0},{5,1},{6,2},{7,3},{8,12},{9,13},{10,... | collective-permute-start | bytes 393224 | tf_op jit(solution)/shard_map/ppermute | solution.py:166
  16.1 7.1 %collective-permute-start.20 = (bf16[16,4096]{1,0:T(8,128)(2,1)S(1)}, bf16[16,4096]{1,0:T(8,128)(2,1)S(1)}, u32[]{:S(2)}, u32[]{:S(2)}) collective-permute-start(bf16[16,4096]{1,0:T(8,128)(2,1)S(1)} %collective-permute-done.18.refs_19_), channel_id=1, source_target_pairs={{0,2},{1,3},{2,0},{3,1},{4,6},{5,7},{6,4},{7,5},{8,10},{9,11},{10,... | collective-permute-start | bytes 393224 | tf_op jit(solution)/shard_map/ppermute | solution.py:166
  19.6 3.5 %collective-permute-start.19 = (bf16[16,4096]{1,0:T(8,128)(2,1)S(1)}, bf16[16,4096]{1,0:T(8,128)(2,1)S(1)}, u32[]{:S(2)}, u32[]{:S(2)}) collective-permute-start(bf16[16,4096]{1,0:T(8,128)(2,1)S(1)} %collective-permute-done.18.refs_19_), channel_id=1, source_target_pairs={{0,1},{1,0},{2,3},{3,2},{4,5},{5,4},{6,7},{7,6},{8,9},{9,8},{10,11... | collective-permute-start | bytes 393224 | tf_op jit(solution)/shard_map/ppermute | solution.py:166
  19.6 6.0 %collective-permute-start.14 = (bf16[16,4096]{1,0:T(8,128)(2,1)S(1)}, bf16[16,4096]{1,0:T(8,128)(2,1)S(1)}, u32[]{:S(2)}, u32[]{:S(2)}) collective-permute-start(bf16[16,4096]{1,0:T(8,128)(2,1)S(1)} %collective-permute-done.10.refs_11_), channel_id=1, source_target_pairs={{0,4},{1,5},{2,6},{3,7},{4,0},{5,1},{6,2},{7,3},{8,12},{9,13},{10,... | collective-permute-start | bytes 393224 | tf_op jit(solution)/shard_map/ppermute | solution.py:166
  21.1 6.3 %collective-permute-start.12 = (bf16[16,4096]{1,0:T(8,128)(2,1)S(1)}, bf16[16,4096]{1,0:T(8,128)(2,1)S(1)}, u32[]{:S(2)}, u32[]{:S(2)}) collective-permute-start(bf16[16,4096]{1,0:T(8,128)(2,1)S(1)} %collective-permute-done.10.refs_11_), channel_id=1, source_target_pairs={{0,2},{1,3},{2,0},{3,1},{4,6},{5,7},{6,4},{7,5},{8,10},{9,11},{10,... | collective-permute-start | bytes 393224 | tf_op jit(solution)/shard_map/ppermute | solution.py:166
  22.6 13.3 %collective-permute-start = (bf16[16,8192]{1,0:T(8,128)(2,1)}, bf16[16,8192]{1,0:T(8,128)(2,1)S(1)}, u32[]{:S(2)}, u32[]{:S(2)}) collective-permute-start(bf16[16,8192]{1,0:T(8,128)(2,1)} %get-tuple-element.10), channel_id=1, source_target_pairs={{0,4},{1,5},{2,6},{3,7},{4,0},{5,1},{6,2},{7,3},{8,12},{9,13},{10,... | collective-permute-start | bytes 786440 | tf_op jit(solution)/shard_map/ppermute | solution.py:166
  23.1 4.3 %collective-permute-start.11 = (bf16[16,4096]{1,0:T(8,128)(2,1)S(1)}, bf16[16,4096]{1,0:T(8,128)(2,1)S(1)}, u32[]{:S(2)}, u32[]{:S(2)}) collective-permute-start(bf16[16,4096]{1,0:T(8,128)(2,1)S(1)} %collective-permute-done.10.refs_11_), channel_id=1, source_target_pairs={{0,1},{1,0},{2,3},{3,2},{4,5},{5,4},{6,7},{7,6},{8,9},{9,8},{10,11... | collective-permute-start | bytes 393224 | tf_op jit(solution)/shard_map/ppermute | solution.py:166
  23.1 10.8 %collective-permute-start.6 = (bf16[16,4096]{1,0:T(8,128)(2,1)S(1)}, bf16[16,4096]{1,0:T(8,128)(2,1)S(1)}, u32[]{:S(2)}, u32[]{:S(2)}) collective-permute-start(bf16[16,4096]{1,0:T(8,128)(2,1)S(1)} %collective-permute-done.2.refs_3_), channel_id=1, source_target_pairs={{0,4},{1,5},{2,6},{3,7},{4,0},{5,1},{6,2},{7,3},{8,12},{9,13},{10,... | collective-permute-start | bytes 393224 | tf_op jit(solution)/shard_map/ppermute | solution.py:166
  25.6 8.3 %collective-permute-start.4 = (bf16[16,4096]{1,0:T(8,128)(2,1)S(1)}, bf16[16,4096]{1,0:T(8,128)(2,1)S(1)}, u32[]{:S(2)}, u32[]{:S(2)}) collective-permute-start(bf16[16,4096]{1,0:T(8,128)(2,1)S(1)} %collective-permute-done.2.refs_3_), channel_id=1, source_target_pairs={{0,2},{1,3},{2,0},{3,1},{4,6},{5,7},{6,4},{7,5},{8,10},{9,11},{10,... | collective-permute-start | bytes 393224 | tf_op jit(solution)/shard_map/ppermute | solution.py:166
  27.5 7.0 %collective-permute-start.3 = (bf16[16,4096]{1,0:T(8,128)(2,1)S(1)}, bf16[16,4096]{1,0:T(8,128)(2,1)S(1)}, u32[]{:S(2)}, u32[]{:S(2)}) collective-permute-start(bf16[16,4096]{1,0:T(8,128)(2,1)S(1)} %collective-permute-done.2.refs_3_), channel_id=1, source_target_pairs={{0,1},{1,0},{2,3},{3,2},{4,5},{5,4},{6,7},{7,6},{8,9},{9,8},{10,11... | collective-permute-start | bytes 393224 | tf_op jit(solution)/shard_map/ppermute | solution.py:166
  27.5 8.5 %collective-permute-start.25 = (bf16[16,4096]{1,0:T(8,128)(2,1)S(1)}, bf16[16,4096]{1,0:T(8,128)(2,1)S(1)}, u32[]{:S(2)}, u32[]{:S(2)}) collective-permute-start(bf16[16,4096]{1,0:T(8,128)(2,1)S(1)} %collective-permute-done.24.refs_25_), channel_id=1, source_target_pairs={{0,1},{1,0},{2,3},{3,2},{4,5},{5,4},{6,7},{7,6},{8,9},{9,8},{10,11... | collective-permute-start | bytes 393224 | tf_op jit(solution)/shard_map/ppermute | solution.py:166
  33.9 2.5 %collective-permute-start.23 = (bf16[16,4096]{1,0:T(8,128)(2,1)S(1)}, bf16[16,4096]{1,0:T(8,128)(2,1)S(1)}, u32[]{:S(2)}, u32[]{:S(2)}) collective-permute-start(bf16[16,4096]{1,0:T(8,128)(2,1)S(1)} %collective-permute-done.22.refs_23_), channel_id=1, source_target_pairs={{0,1},{1,0},{2,3},{3,2},{4,5},{5,4},{6,7},{7,6},{8,9},{9,8},{10,11... | collective-permute-start | bytes 393224 | tf_op jit(solution)/shard_map/ppermute | solution.py:166
  33.9 3.1 %collective-permute-start.21 = (bf16[16,4096]{1,0:T(8,128)(2,1)S(1)}, bf16[16,4096]{1,0:T(8,128)(2,1)S(1)}, u32[]{:S(2)}, u32[]{:S(2)}) collective-permute-start(bf16[16,4096]{1,0:T(8,128)(2,1)S(1)} %collective-permute-done.20.refs_21_), channel_id=1, source_target_pairs={{0,1},{1,0},{2,3},{3,2},{4,5},{5,4},{6,7},{7,6},{8,9},{9,8},{10,11... | collective-permute-start | bytes 393224 | tf_op jit(solution)/shard_map/ppermute | solution.py:166
  34.4 6.3 %collective-permute-start.16 = (bf16[16,4096]{1,0:T(8,128)(2,1)S(1)}, bf16[16,4096]{1,0:T(8,128)(2,1)S(1)}, u32[]{:S(2)}, u32[]{:S(2)}) collective-permute-start(bf16[16,4096]{1,0:T(8,128)(2,1)S(1)} %collective-permute-done.14.refs_15_), channel_id=1, source_target_pairs={{0,2},{1,3},{2,0},{3,1},{4,6},{5,7},{6,4},{7,5},{8,10},{9,11},{10,... | collective-permute-start | bytes 393224 | tf_op jit(solution)/shard_map/ppermute | solution.py:166
  35.9 4.8 %collective-permute-start.15 = (bf16[16,4096]{1,0:T(8,128)(2,1)S(1)}, bf16[16,4096]{1,0:T(8,128)(2,1)S(1)}, u32[]{:S(2)}, u32[]{:S(2)}) collective-permute-start(bf16[16,4096]{1,0:T(8,128)(2,1)S(1)} %collective-permute-done.14.refs_15_), channel_id=1, source_target_pairs={{0,1},{1,0},{2,3},{3,2},{4,5},{5,4},{6,7},{7,6},{8,9},{9,8},{10,11... | collective-permute-start | bytes 393224 | tf_op jit(solution)/shard_map/ppermute | solution.py:166
  35.9 5.3 %collective-permute-start.13 = (bf16[16,4096]{1,0:T(8,128)(2,1)S(1)}, bf16[16,4096]{1,0:T(8,128)(2,1)S(1)}, u32[]{:S(2)}, u32[]{:S(2)}) collective-permute-start(bf16[16,4096]{1,0:T(8,128)(2,1)S(1)} %collective-permute-done.12.refs_13_), channel_id=1, source_target_pairs={{0,1},{1,0},{2,3},{3,2},{4,5},{5,4},{6,7},{7,6},{8,9},{9,8},{10,11... | collective-permute-start | bytes 393224 | tf_op jit(solution)/shard_map/ppermute | solution.py:166
  36.5 6.3 %collective-permute-start.8 = (bf16[16,4096]{1,0:T(8,128)(2,1)S(1)}, bf16[16,4096]{1,0:T(8,128)(2,1)S(1)}, u32[]{:S(2)}, u32[]{:S(2)}) collective-permute-start(bf16[16,4096]{1,0:T(8,128)(2,1)S(1)} %collective-permute-done.6.refs_7_), channel_id=1, source_target_pairs={{0,2},{1,3},{2,0},{3,1},{4,6},{5,7},{6,4},{7,5},{8,10},{9,11},{10,... | collective-permute-start | bytes 393224 | tf_op jit(solution)/shard_map/ppermute | solution.py:166
  37.0 7.1 %collective-permute-start.1 = (bf16[16,8192]{1,0:T(8,128)(2,1)S(1)}, bf16[16,8192]{1,0:T(8,128)(2,1)S(1)}, u32[]{:S(2)}, u32[]{:S(2)}) collective-permute-start(bf16[16,8192]{1,0:T(8,128)(2,1)S(1)} %collective-permute-done.refs_1_), channel_id=1, source_target_pairs={{0,1},{1,0},{2,3},{3,2},{4,5},{5,4},{6,7},{7,6},{8,9},{9,8},{10,11... | collective-permute-start | bytes 786440 | tf_op jit(solution)/shard_map/ppermute | solution.py:166
  40.7 2.0 %collective-permute-start.7 = (bf16[16,4096]{1,0:T(8,128)(2,1)S(1)}, bf16[16,4096]{1,0:T(8,128)(2,1)S(1)}, u32[]{:S(2)}, u32[]{:S(2)}) collective-permute-start(bf16[16,4096]{1,0:T(8,128)(2,1)S(1)} %collective-permute-done.6.refs_7_), channel_id=1, source_target_pairs={{0,1},{1,0},{2,3},{3,2},{4,5},{5,4},{6,7},{7,6},{8,9},{9,8},{10,11... | collective-permute-start | bytes 393224 | tf_op jit(solution)/shard_map/ppermute | solution.py:166
  40.7 2.0 %collective-permute-start.5 = (bf16[16,4096]{1,0:T(8,128)(2,1)S(1)}, bf16[16,4096]{1,0:T(8,128)(2,1)S(1)}, u32[]{:S(2)}, u32[]{:S(2)}) collective-permute-start(bf16[16,4096]{1,0:T(8,128)(2,1)S(1)} %collective-permute-done.4.refs_5_), channel_id=1, source_target_pairs={{0,1},{1,0},{2,3},{3,2},{4,5},{5,4},{6,7},{7,6},{8,9},{9,8},{10,11... | collective-permute-start | bytes 393224 | tf_op jit(solution)/shard_map/ppermute | solution.py:166
  41.2 1.5 %collective-permute-start.17 = (bf16[16,4096]{1,0:T(8,128)(2,1)S(1)}, bf16[16,4096]{1,0:T(8,128)(2,1)S(1)}, u32[]{:S(2)}, u32[]{:S(2)}) collective-permute-start(bf16[16,4096]{1,0:T(8,128)(2,1)S(1)} %collective-permute-done.16.refs_17_), channel_id=1, source_target_pairs={{0,1},{1,0},{2,3},{3,2},{4,5},{5,4},{6,7},{7,6},{8,9},{9,8},{10,11... | collective-permute-start | bytes 393224 | tf_op jit(solution)/shard_map/ppermute | solution.py:166
  42.7 1.3 %collective-permute-start.9 = (bf16[16,4096]{1,0:T(8,128)(2,1)S(1)}, bf16[16,4096]{1,0:T(8,128)(2,1)S(1)}, u32[]{:S(2)}, u32[]{:S(2)}) collective-permute-start(bf16[16,4096]{1,0:T(8,128)(2,1)S(1)} %collective-permute-done.8.refs_9_), channel_id=1, source_target_pairs={{0,1},{1,0},{2,3},{3,2},{4,5},{5,4},{6,7},{7,6},{8,9},{9,8},{10,11... | collective-permute-start | bytes 393224 | tf_op jit(solution)/shard_map/ppermute | solution.py:166
  44.1 2.8 %copy-start = (bf16[12,12,16384]{2,1,0:T(8,128)(2,1)S(1)}, bf16[12,12,16384]{2,1,0:T(8,128)(2,1)}, u32[]{:S(2)}) copy-start(bf16[12,12,16384]{2,1,0:T(8,128)(2,1)} %refs_27_.1) | copy-start | bytes 14155780
  46.9 1.0 %copy-start.1 = (bf16[16,16384]{1,0:T(8,128)(2,1)S(1)}, bf16[16,16384]{1,0:T(8,128)(2,1)}, u32[]{:S(2)}) copy-start(bf16[16,16384]{1,0:T(8,128)(2,1)} %get-tuple-element.9.refs_0_) | copy-start | bytes 1572868
